TPU v7x, 32 devices: a whole 2x2x4 slice. The times are simulated.
32 devices in a mesh: kpt: 4 (over y, x), pw: 8 (over z, core).
Axes of the slice: x: 2, y: 2, z: 4, core: 2. Of those that a mesh axis runs over, the one named last changes fastest.
Arguments:
- energies: float32 [16, 512], P('kpt', 'pw'), may hold values from 0.5 to 3
- current: float32 [2, 16, 512], P(None, 'kpt', 'pw'), may hold values from -40 to 40
- previous: float32 [2, 16, 512], P(None, 'kpt', 'pw'), may hold values from -6 to 6
- previous_beta: float32 [2], replicated, may hold values from 0.5 to 2
- pair_left: bfloat16 [16, 512, 4096], P('kpt', None, 'pw'), may hold values from -0.09375 to 0.09375
- pair_right: bfloat16 [16, 512, 4096], P('kpt', None, 'pw'), may hold values from -0.25 to 0.25
- screened: bfloat16 [16, 4096, 4096], P('kpt', 'pw'), may hold values from -0.0234375 to 0.0234375
- momentum_index: int32 [16, 16], replicated, may hold values from 0 to 15, each once within a row
Outputs:
- last_vector: float32 [2, 16, 512], P(None, 'kpt', 'pw')
- prior_vector: float32 [2, 16, 512], P(None, 'kpt', 'pw')
- alpha_terms: float32 [2, 3], replicated
- beta_terms: float32 [2, 3], replicated
Inputs may be any that keep to these rules, and one draw needn't show every extreme that they name: Each row of momentum_index names every index from 0 to 15 once.
All inputs are finite; a program needn't handle non-finite values.
Results may differ from a plain program's by a relative error of at most 0.003.
Values may be sent and summed in bfloat16 or wider, within the bound.
A program may use at most 128 MiB of HBM per device.

v0:
```python
import jax
import jax.numpy as jnp
from jax import lax
from jax.sharding import PartitionSpec as P

STEPS = 3
epsilon = 1e-06


def screened_images(density, screened):
    kpoint_rows = lax.all_gather(density, "kpt", axis=0, tiled=True)
    return jnp.einsum(
        "qsg,kvg->qkvs",
        screened,
        lax.all_gather(kpoint_rows, "pw", axis=2, tiled=True),
        preferred_element_type=jnp.float32,
    )


def on_device(
    energies, current, previous, previous_beta, pair_left, pair_right, screened, momentum_index
):
    kpoint_total = momentum_index.shape[0]
    band_total = pair_left.shape[1]
    entries = kpoint_total * band_total
    qcount = screened.shape[0]
    qpoints = lax.axis_index("kpt") * qcount + jnp.arange(qcount, dtype=jnp.int32)
    selector = (momentum_index[None, :, :] == qpoints[:, None, None]).astype(jnp.float32)
    vector, earlier, levels = (current, previous, energies)
    beta_before = previous_beta
    alpha_list = []
    beta_list = []
    for turn_index in range(STEPS):
        rounded = vector.astype(jnp.bfloat16)
        rounded = lax.all_gather(rounded, "pw", axis=2, tiled=True)
        density = jnp.einsum(
            "kcg,vkc->kvg", pair_right, rounded, preferred_element_type=jnp.float32
        ).astype(jnp.bfloat16)
        images = screened_images(density, screened)
        partial_field = jnp.einsum(
            "qjk,qkvs->jvs",
            selector,
            images,
            precision=lax.Precision.HIGHEST,
            preferred_element_type=jnp.float32,
        )
        potential = lax.psum_scatter(partial_field, "kpt", scatter_dimension=0, tiled=True).astype(
            jnp.bfloat16
        )
        partial_direct = jnp.einsum(
            "kcs,kvs->vkc", pair_left, potential, preferred_element_type=jnp.float32
        )
        direct = lax.psum_scatter(partial_direct, "pw", scatter_dimension=2, tiled=True)
        applied = levels[None] * vector - direct - beta_before[:, None, None] * earlier
        vector_own = vector
        cross_sum, square_sum, vector_sum = lax.psum(
            (
                jnp.sum(vector_own * applied, axis=(1, 2)),
                jnp.sum(applied * applied, axis=(1, 2)),
                jnp.sum(vector_own * vector_own, axis=(1, 2)),
            ),
            ("kpt", "pw"),
        )
        alpha_now = cross_sum / entries
        mean_square = (
            square_sum / entries
            - 2.0 * alpha_now * (cross_sum / entries)
            + alpha_now * alpha_now * (vector_sum / entries)
        )
        beta_now = jnp.sqrt(mean_square + epsilon)
        residual = applied - alpha_now[:, None, None] * vector
        earlier = vector
        vector = residual / beta_now[:, None, None]
        beta_before = beta_now
        alpha_list.append(alpha_now)
        beta_list.append(beta_now)
    return (vector, earlier, jnp.stack(alpha_list, axis=1), jnp.stack(beta_list, axis=1))


def solution(mesh):
    return jax.shard_map(
        on_device,
        mesh=mesh,
        in_specs=(
            P("kpt", "pw"),
            P(None, "kpt", "pw"),
            P(None, "kpt", "pw"),
            P(),
            P("kpt", None, "pw"),
            P("kpt", None, "pw"),
            P("kpt", "pw", None),
            P(),
        ),
        out_specs=(P(None, "kpt", "pw"), P(None, "kpt", "pw"), P(), P()),
        check_vma=False,
    )
```

profile of v0, /device:TPU:10, one launch (start us, length us, event | category | flops | bytes accessed | tf_op | source)
XLA Modules:
  0.0 434.7 jit_solution(2461469843560152316)
XLA Ops:
  8.2 14.4 %all_gather.27 = bf16[2,4,512]{1,0,2:T(2,128)(2,1)S(1)} all-gather(bf16[2,4,64]{1,0,2:T(2,128)(2,1)S(1)} %copy.33), channel_id=1, replica_groups=mesh['kpt'=4,'pw'=8] {'pw'}, dimensions={2}, use_global_device_ids=true | all-gather | bytes 9216 | tf_op jit(solution)/shard_map/all_gather | solution.py:35
  23.2 8.2 %all_gather.28 = bf16[16,2,512]{2,1,0:T(2,128)(2,1)S(1)} all-gather(bf16[4,2,512]{2,1,0:T(2,128)(2,1)S(1)} %convolution_convert_fusion.2), channel_id=1, replica_groups=mesh['kpt'=4,'pw'=8] {'kpt'}, dimensions={0}, use_global_device_ids=true | all-gather | bytes 40960 | tf_op jit(solution)/shard_map/all_gather | solution.py:11
  31.4 14.3 %all_gather.29 = bf16[16,2,4096]{2,0,1:T(8,128)(2,1)S(1)} all-gather(bf16[16,2,512]{2,0,1:T(8,128)(2,1)S(1)} %copy.35), channel_id=1, replica_groups=mesh['kpt'=4,'pw'=8] {'pw'}, dimensions={2}, use_global_device_ids=true | all-gather | bytes 294912 | tf_op jit(solution)/shard_map/all_gather | solution.py:15
  45.6 10.8 %fusion.6 = f32[4,16,2,512]{3,1,0,2:T(8,128)S(1)} fusion(bf16[4,512,4096]{2,1,0:T(8,128)(2,1)} %param.14, bf16[16,2,4096]{2,0,1:T(8,128)(2,1)S(1)} %all_gather.29), kind=kOutput, calls=%fused_computation.6 | convolution fusion | flops 536870912 | bytes 17301504 | tf_op jit(solution)/shard_map/qsg,kvg->qkvs/dot_general | solution.py:12
  56.9 15.0 %all-reduce = bf16[16,2,512]{2,1,0:T(2,128)(2,1)S(1)} all-reduce(f32[16,2,512]{2,1,0:T(2,128)S(1)} %copy.36), channel_id=2, replica_groups=mesh['kpt'=4,'pw'=8] {'kpt'}, use_global_device_ids=true, to_apply=%region_0.0.clone | all-reduce | flops 16384 | bytes 98304
  73.2 2.2 convolution_bitcast_fusion.5
  77.1 28.3 %reduce-scatter.10.cloned.1.call-done = f32[64,8]{1,0:T(8,128)} async-done(((f32[512,8]{1,0:T(8,128)}), f32[64,8]{1,0:T(8,128)}) %reduce-scatter.10.cloned.1.call-update) | async-done | bytes 2064
  106.6 43.5 %all-reduce.5 = (f32[2]{0:T(128)S(1)}, f32[2]{0:T(128)S(1)}, f32[2]{0:T(128)S(1)}) all-reduce(f32[2]{0:T(128)S(1)} %get-tuple-element.24, f32[2]{0:T(128)S(1)} %get-tuple-element.23, f32[2]{0:T(128)S(1)} %get-tuple-element.22), channel_id=1, replica_groups=mesh['kpt'=4,'pw'=8] {'kpt','pw'}, use_global_device_ids=true, to_apply=%region_7.0 | all-reduce | flops 6 | bytes 48 | tf_op jit(solution)/shard_map/psum | solution.py:56
  150.4 12.4 %all_gather.30 = bf16[2,4,512]{1,0,2:T(2,128)(2,1)S(1)} all-gather(bf16[2,4,64]{1,0,2:T(2,128)(2,1)S(1)} %copy.38), channel_id=1, replica_groups=mesh['kpt'=4,'pw'=8] {'pw'}, dimensions={2}, use_global_device_ids=true | all-gather | bytes 9216 | tf_op jit(solution)/shard_map/all_gather | solution.py:35
  163.3 7.2 %all_gather.31 = bf16[16,2,512]{2,1,0:T(2,128)(2,1)S(1)} all-gather(bf16[4,2,512]{2,1,0:T(2,128)(2,1)S(1)} %convolution_convert_fusion.1), channel_id=1, replica_groups=mesh['kpt'=4,'pw'=8] {'kpt'}, dimensions={0}, use_global_device_ids=true | all-gather | bytes 40960 | tf_op jit(solution)/shard_map/all_gather | solution.py:11
  170.5 14.4 %all_gather.32 = bf16[16,2,4096]{2,0,1:T(8,128)(2,1)S(1)} all-gather(bf16[16,2,512]{2,0,1:T(8,128)(2,1)S(1)} %copy.40), channel_id=1, replica_groups=mesh['kpt'=4,'pw'=8] {'pw'}, dimensions={2}, use_global_device_ids=true | all-gather | bytes 294912 | tf_op jit(solution)/shard_map/all_gather | solution.py:15
  184.9 10.8 %fusion.9 = f32[4,16,2,512]{3,1,0,2:T(8,128)S(1)} fusion(bf16[4,512,4096]{2,1,0:T(8,128)(2,1)} %param.14, bf16[16,2,4096]{2,0,1:T(8,128)(2,1)S(1)} %all_gather.32), kind=kOutput, calls=%fused_computation.7 | convolution fusion | flops 536870912 | bytes 17301504 | tf_op jit(solution)/shard_map/qsg,kvg->qkvs/dot_general | solution.py:12
  196.2 15.7 %all-reduce.1 = bf16[16,2,512]{2,1,0:T(2,128)(2,1)S(1)} all-reduce(f32[16,2,512]{2,1,0:T(2,128)S(1)} %copy.41), channel_id=4, replica_groups=mesh['kpt'=4,'pw'=8] {'kpt'}, use_global_device_ids=true, to_apply=%region_8.0.clone | all-reduce | flops 16384 | bytes 98304
  211.8 2.2 convolution_bitcast_fusion.4
  215.8 27.7 %reduce-scatter.12.cloned.1.call-done = f32[64,8]{1,0:T(8,128)} async-done(((f32[512,8]{1,0:T(8,128)}), f32[64,8]{1,0:T(8,128)}) %reduce-scatter.12.cloned.1.call-update) | async-done | bytes 2064
  244.7 43.5 %all-reduce.4 = (f32[2]{0:T(128)S(1)}, f32[2]{0:T(128)S(1)}, f32[2]{0:T(128)S(1)}) all-reduce(f32[2]{0:T(128)S(1)} %get-tuple-element.21, f32[2]{0:T(128)S(1)} %get-tuple-element.20, f32[2]{0:T(128)S(1)} %get-tuple-element.19), channel_id=1, replica_groups=mesh['kpt'=4,'pw'=8] {'kpt','pw'}, use_global_device_ids=true, to_apply=%region_15.0 | all-reduce | flops 6 | bytes 48 | tf_op jit(solution)/shard_map/psum | solution.py:56
  288.3 12.4 %all_gather.33 = bf16[2,4,512]{1,0,2:T(2,128)(2,1)S(1)} all-gather(bf16[2,4,64]{1,0,2:T(2,128)(2,1)S(1)} %copy.43), channel_id=1, replica_groups=mesh['kpt'=4,'pw'=8] {'pw'}, dimensions={2}, use_global_device_ids=true | all-gather | bytes 9216 | tf_op jit(solution)/shard_map/all_gather | solution.py:35
  301.3 7.3 %all_gather.34 = bf16[16,2,512]{2,1,0:T(2,128)(2,1)S(1)} all-gather(bf16[4,2,512]{2,1,0:T(2,128)(2,1)S(1)} %convolution_convert_fusion), channel_id=1, replica_groups=mesh['kpt'=4,'pw'=8] {'kpt'}, dimensions={0}, use_global_device_ids=true | all-gather | bytes 40960 | tf_op jit(solution)/shard_map/all_gather | solution.py:11
  308.6 14.2 %all_gather.35 = bf16[16,2,4096]{2,0,1:T(8,128)(2,1)S(1)} all-gather(bf16[16,2,512]{2,0,1:T(8,128)(2,1)S(1)} %copy.45), channel_id=1, replica_groups=mesh['kpt'=4,'pw'=8] {'pw'}, dimensions={2}, use_global_device_ids=true | all-gather | bytes 294912 | tf_op jit(solution)/shard_map/all_gather | solution.py:15
  322.8 10.8 %fusion.12 = f32[4,16,2,512]{3,1,0,2:T(8,128)S(1)} fusion(bf16[4,512,4096]{2,1,0:T(8,128)(2,1)} %param.14, bf16[16,2,4096]{2,0,1:T(8,128)(2,1)S(1)} %all_gather.35), kind=kOutput, calls=%fused_computation.8 | convolution fusion | flops 536870912 | bytes 17301504 | tf_op jit(solution)/shard_map/qsg,kvg->qkvs/dot_general | solution.py:12
  334.1 15.6 %all-reduce.2 = bf16[16,2,512]{2,1,0:T(2,128)(2,1)S(1)} all-reduce(f32[16,2,512]{2,1,0:T(2,128)S(1)} %copy.46), channel_id=6, replica_groups=mesh['kpt'=4,'pw'=8] {'kpt'}, use_global_device_ids=true, to_apply=%region_16.0.clone | all-reduce | flops 16384 | bytes 98304
  349.6 2.2 convolution_bitcast_fusion.3
  353.5 28.0 %reduce-scatter.14.cloned.1.call-done = f32[64,8]{1,0:T(8,128)} async-done(((f32[512,8]{1,0:T(8,128)}), f32[64,8]{1,0:T(8,128)}) %reduce-scatter.14.cloned.1.call-update) | async-done | bytes 2064
  382.7 43.5 %all-reduce.3 = (f32[2]{0:T(128)S(1)}, f32[2]{0:T(128)S(1)}, f32[2]{0:T(128)S(1)}) all-reduce(f32[2]{0:T(128)S(1)} %get-tuple-element.18, f32[2]{0:T(128)S(1)} %get-tuple-element.17, f32[2]{0:T(128)S(1)} %get-tuple-element.16), channel_id=1, replica_groups=mesh['kpt'=4,'pw'=8] {'kpt','pw'}, use_global_device_ids=true, to_apply=%region_23.0 | all-reduce | flops 6 | bytes 48 | tf_op jit(solution)/shard_map/psum | solution.py:56
  (68 shorter events, 15.3 us)
Async XLA Ops:
  7.2 15.6 %copy-start = (bf16[4,512,512]{2,1,0:T(8,128)(2,1)S(1)}, bf16[4,512,512]{2,1,0:T(8,128)(2,1)}, u32[]{:S(2)}) copy-start(bf16[4,512,512]{2,1,0:T(8,128)(2,1)} %param.13) | copy-start | bytes 6291460
  7.2 98.2 %reduce-scatter.10.cloned.1.call-start = ((), (), s32[]{:S(2)}) async-start(), calls=%async_computation.3 | async-start | bytes 294912
  45.6 10.8 %copy-start.1 = (s32[16,16]{1,0:T(8,128)S(1)}, s32[16,16]{1,0:T(8,128)}, u32[]{:S(2)}) copy-start(s32[16,16]{1,0:T(8,128)} %param.15) | copy-start | bytes 3076
  45.6 26.3 %copy-start.7 = (u32[32]{0:T(128)S(1)}, u32[32]{0:T(128)}, u32[]{:S(2)}) copy-start(u32[32]{0:T(128)} %constant.29) | copy-start | bytes 388
  73.2 33.2 %copy-start.2 = (f32[2,4,64]{2,1,0:T(4,128)S(1)}, f32[2,4,64]{2,1,0:T(4,128)}, u32[]{:S(2)}) copy-start(f32[2,4,64]{2,1,0:T(4,128)} %param.9) | copy-start | bytes 6148
  73.2 33.2 %copy-start.4 = (f32[4,64]{1,0:T(4,128)S(1)}, f32[4,64]{1,0:T(4,128)}, u32[]{:S(2)}) copy-start(f32[4,64]{1,0:T(4,128)} %param.8) | copy-start | bytes 3076
  73.2 33.2 %copy-start.5 = (f32[2,4,64]{2,1,0:T(4,128)S(1)}, f32[2,4,64]{2,1,0:T(4,128)}, u32[]{:S(2)}) copy-start(f32[2,4,64]{2,1,0:T(4,128)} %param.10) | copy-start | bytes 6148
  73.2 33.2 %copy-start.6 = (f32[2]{0:T(128)S(1)}, f32[2]{0:T(128)}, u32[]{:S(2)}) copy-start(f32[2]{0:T(128)} %param.11) | copy-start | bytes 28
  77.1 166.4 %reduce-scatter.12.cloned.1.call-start = ((), (), s32[]{:S(2)}) async-start(), calls=%async_computation.4 | async-start | bytes 294912
  215.7 165.8 %reduce-scatter.14.cloned.1.call-start = ((), (), s32[]{:S(2)}) async-start(), calls=%async_computation.5 | async-start | bytes 294912
  288.2 139.3 %copy-start.3 = (f32[2,4,64]{2,1,0:T(4,128)}, f32[2,4,64]{2,1,0:T(4,128)S(1)}, u32[]{:S(2)}) copy-start(f32[2,4,64]{2,1,0:T(4,128)S(1)} %get-tuple-element.36) | copy-start | bytes 6148
Sparse Core Ops, SparseCore 0:
  77.2 28.1 reduce-scatter.9
  215.8 27.6 reduce-scatter.11
  353.6 27.8 reduce-scatter.13
where the time goes:
time: 436 us; the launch traced here: 435 us
  blocking collectives  282 us (65%)
  waiting for transfers between devices  84.1 us (19%)
  matrix products  41.3 us (9%)
  between operations  14.7 us (3%)
  local copies, waits for them, and re-layouts  10.7 us (2%)
    psum x3, blocking collectives, on_device(): lax.psum((jnp.sum(vector_own * applied, axis=(1, 2)), jnp.sum(applied * a...  130 us
    unnamed x6, waiting for transfers between devices  84.1 us
    unnamed x3, blocking collectives  46.3 us
    all_gather x3, blocking collectives, screened_images(): lax.all_gather(kpoint_rows, 'pw', axis=2, tiled=True)  42.9 us
    all_gather x3, blocking collectives, on_device(): rounded = lax.all_gather(rounded, 'pw', axis=2, tiled=True)  39.2 us
    dot_general x3, matrix products, screened_images(): jnp.einsum('qsg,kvg->qkvs', screened, lax.all_gather(kpoint_rows, 'pw', a...  32.4 us
    all_gather x3, blocking collectives, screened_images(): kpoint_rows = lax.all_gather(density, 'kpt', axis=0, tiled=True)  22.8 us
    unnamed x28, local copies, waits for them, and re-layouts  9.34 us
  transfers between devices with their start and end apart: 3, of which 3 were waited for; matrix products, arithmetic and copies ran while one was open for 0% of the time, Pallas kernels for 0%

commit v1 on v0

--- a/solution.py
+++ b/solution.py
@@ -54,12 +54,15 @@
         applied = levels[None] * vector - direct - beta_before[:, None, None] * earlier
         vector_own = vector
         cross_sum, square_sum, vector_sum = lax.psum(
-            (
-                jnp.sum(vector_own * applied, axis=(1, 2)),
-                jnp.sum(applied * applied, axis=(1, 2)),
-                jnp.sum(vector_own * vector_own, axis=(1, 2)),
+            lax.psum(
+                (
+                    jnp.sum(vector_own * applied, axis=(1, 2)),
+                    jnp.sum(applied * applied, axis=(1, 2)),
+                    jnp.sum(vector_own * vector_own, axis=(1, 2)),
+                ),
+                "kpt",
             ),
-            ("kpt", "pw"),
+            "pw",
         )
         alpha_now = cross_sum / entries
         mean_square = (

time: 436 us -> 386 us (0.89)
  the two profiles are of different devices: /device:TPU:10 before, /device:TPU:0 now
where the time goes in v1:
time: 386 us; the launch traced here: 385 us
  blocking collectives  229 us (59%)
  waiting for transfers between devices  87.3 us (23%)
  matrix products  41.3 us (11%)
  between operations  14.7 us (4%)
  local copies, waits for them, and re-layouts  10.7 us (3%)
    unnamed x6, waiting for transfers between devices  87.3 us
    unnamed x3, blocking collectives  48.4 us
    all_gather x3, blocking collectives, on_device(): rounded = lax.all_gather(rounded, 'pw', axis=2, tiled=True)  44.3 us
    all_gather x3, blocking collectives, screened_images(): lax.all_gather(kpoint_rows, 'pw', axis=2, tiled=True)  43 us
    psum x3, blocking collectives, on_device(): lax.psum(lax.psum((jnp.sum(vector_own * applied, axis=(1, 2)), jnp.sum(ap...  40.8 us
    dot_general x3, matrix products, screened_images(): jnp.einsum('qsg,kvg->qkvs', screened, lax.all_gather(kpoint_rows, 'pw', a...  32.4 us
    psum x3, blocking collectives, on_device(): lax.psum((jnp.sum(vector_own * applied, axis=(1, 2)), jnp.sum(applied * a...  29.5 us
    all_gather x3, blocking collectives, screened_images(): kpoint_rows = lax.all_gather(density, 'kpt', axis=0, tiled=True)  22.7 us
  transfers between devices with their start and end apart: 3, of which 3 were waited for; matrix products, arithmetic and copies ran while one was open for 0% of the time, Pallas kernels for 0%

profile of v1, /device:TPU:0, one launch (start us, length us, event | category | flops | bytes accessed | tf_op | source)
XLA Modules:
  0.0 385.0 jit_solution(17494946835726596548)
XLA Ops:
  8.2 15.9 %all_gather.27 = bf16[2,4,512]{1,0,2:T(2,128)(2,1)S(1)} all-gather(bf16[2,4,64]{1,0,2:T(2,128)(2,1)S(1)} %copy.33), channel_id=1, replica_groups=mesh['kpt'=4,'pw'=8] {'pw'}, dimensions={2}, use_global_device_ids=true | all-gather | bytes 9216 | tf_op jit(solution)/shard_map/all_gather | solution.py:35
  24.7 8.2 %all_gather.28 = bf16[16,2,512]{2,1,0:T(2,128)(2,1)S(1)} all-gather(bf16[4,2,512]{2,1,0:T(2,128)(2,1)S(1)} %convolution_convert_fusion.2), channel_id=1, replica_groups=mesh['kpt'=4,'pw'=8] {'kpt'}, dimensions={0}, use_global_device_ids=true | all-gather | bytes 40960 | tf_op jit(solution)/shard_map/all_gather | solution.py:11
  32.9 14.3 %all_gather.29 = bf16[16,2,4096]{2,0,1:T(8,128)(2,1)S(1)} all-gather(bf16[16,2,512]{2,0,1:T(8,128)(2,1)S(1)} %copy.35), channel_id=1, replica_groups=mesh['kpt'=4,'pw'=8] {'pw'}, dimensions={2}, use_global_device_ids=true | all-gather | bytes 294912 | tf_op jit(solution)/shard_map/all_gather | solution.py:15
  47.2 10.8 %fusion.6 = f32[4,16,2,512]{3,1,0,2:T(8,128)S(1)} fusion(bf16[4,512,4096]{2,1,0:T(8,128)(2,1)} %param.14, bf16[16,2,4096]{2,0,1:T(8,128)(2,1)S(1)} %all_gather.29), kind=kOutput, calls=%fused_computation.6 | convolution fusion | flops 536870912 | bytes 17301504 | tf_op jit(solution)/shard_map/qsg,kvg->qkvs/dot_general | solution.py:12
  58.4 16.0 %all-reduce = bf16[16,2,512]{2,1,0:T(2,128)(2,1)S(1)} all-reduce(f32[16,2,512]{2,1,0:T(2,128)S(1)} %copy.36), channel_id=2, replica_groups=mesh['kpt'=4,'pw'=8] {'kpt'}, use_global_device_ids=true, to_apply=%region_0.0.clone | all-reduce | flops 16384 | bytes 98304
  79.7 31.0 %reduce-scatter.10.cloned.1.call-done = f32[64,8]{1,0:T(8,128)} async-done(((f32[512,8]{1,0:T(8,128)}), f32[64,8]{1,0:T(8,128)}) %reduce-scatter.10.cloned.1.call-update) | async-done | bytes 2064
  111.9 9.8 %all-reduce.8 = (f32[2]{0:T(128)S(1)}, f32[2]{0:T(128)S(1)}, f32[2]{0:T(128)S(1)}) all-reduce(f32[2]{0:T(128)S(1)} %get-tuple-element.24, f32[2]{0:T(128)S(1)} %get-tuple-element.23, f32[2]{0:T(128)S(1)} %get-tuple-element.22), channel_id=1, replica_groups=mesh['kpt'=4,'pw'=8] {'kpt'}, use_global_device_ids=true, to_apply=%region_9.0 | all-reduce | flops 6 | bytes 48 | tf_op jit(solution)/shard_map/psum | solution.py:57
  121.7 13.6 %all-reduce.5 = (f32[2]{0:T(128)S(1)}, f32[2]{0:T(128)S(1)}, f32[2]{0:T(128)S(1)}) all-reduce(f32[2]{0:T(128)S(1)} %get-tuple-element.40, f32[2]{0:T(128)S(1)} %get-tuple-element.41, f32[2]{0:T(128)S(1)} %get-tuple-element.42), channel_id=1, replica_groups=mesh['kpt'=4,'pw'=8] {'pw'}, use_global_device_ids=true, to_apply=%region_10.0 | all-reduce | flops 6 | bytes 48 | tf_op jit(solution)/shard_map/psum | solution.py:56
  135.6 14.2 %all_gather.30 = bf16[2,4,512]{1,0,2:T(2,128)(2,1)S(1)} all-gather(bf16[2,4,64]{1,0,2:T(2,128)(2,1)S(1)} %copy.38), channel_id=1, replica_groups=mesh['kpt'=4,'pw'=8] {'pw'}, dimensions={2}, use_global_device_ids=true | all-gather | bytes 9216 | tf_op jit(solution)/shard_map/all_gather | solution.py:35
  150.3 7.3 %all_gather.31 = bf16[16,2,512]{2,1,0:T(2,128)(2,1)S(1)} all-gather(bf16[4,2,512]{2,1,0:T(2,128)(2,1)S(1)} %convolution_convert_fusion.1), channel_id=1, replica_groups=mesh['kpt'=4,'pw'=8] {'kpt'}, dimensions={0}, use_global_device_ids=true | all-gather | bytes 40960 | tf_op jit(solution)/shard_map/all_gather | solution.py:11
  157.6 14.4 %all_gather.32 = bf16[16,2,4096]{2,0,1:T(8,128)(2,1)S(1)} all-gather(bf16[16,2,512]{2,0,1:T(8,128)(2,1)S(1)} %copy.40), channel_id=1, replica_groups=mesh['kpt'=4,'pw'=8] {'pw'}, dimensions={2}, use_global_device_ids=true | all-gather | bytes 294912 | tf_op jit(solution)/shard_map/all_gather | solution.py:15
  172.0 10.8 %fusion.9 = f32[4,16,2,512]{3,1,0,2:T(8,128)S(1)} fusion(bf16[4,512,4096]{2,1,0:T(8,128)(2,1)} %param.14, bf16[16,2,4096]{2,0,1:T(8,128)(2,1)S(1)} %all_gather.32), kind=kOutput, calls=%fused_computation.7 | convolution fusion | flops 536870912 | bytes 17301504 | tf_op jit(solution)/shard_map/qsg,kvg->qkvs/dot_general | solution.py:12
  183.2 16.2 %all-reduce.1 = bf16[16,2,512]{2,1,0:T(2,128)(2,1)S(1)} all-reduce(f32[16,2,512]{2,1,0:T(2,128)S(1)} %copy.41), channel_id=4, replica_groups=mesh['kpt'=4,'pw'=8] {'kpt'}, use_global_device_ids=true, to_apply=%region_11.0.clone | all-reduce | flops 16384 | bytes 98304
  203.3 28.1 %reduce-scatter.12.cloned.1.call-done = f32[64,8]{1,0:T(8,128)} async-done(((f32[512,8]{1,0:T(8,128)}), f32[64,8]{1,0:T(8,128)}) %reduce-scatter.12.cloned.1.call-update) | async-done | bytes 2064
  232.6 9.8 %all-reduce.7 = (f32[2]{0:T(128)S(1)}, f32[2]{0:T(128)S(1)}, f32[2]{0:T(128)S(1)}) all-reduce(f32[2]{0:T(128)S(1)} %get-tuple-element.21, f32[2]{0:T(128)S(1)} %get-tuple-element.20, f32[2]{0:T(128)S(1)} %get-tuple-element.19), channel_id=1, replica_groups=mesh['kpt'=4,'pw'=8] {'kpt'}, use_global_device_ids=true, to_apply=%region_20.0 | all-reduce | flops 6 | bytes 48 | tf_op jit(solution)/shard_map/psum | solution.py:57
  242.4 13.6 %all-reduce.4 = (f32[2]{0:T(128)S(1)}, f32[2]{0:T(128)S(1)}, f32[2]{0:T(128)S(1)}) all-reduce(f32[2]{0:T(128)S(1)} %get-tuple-element.37, f32[2]{0:T(128)S(1)} %get-tuple-element.38, f32[2]{0:T(128)S(1)} %get-tuple-element.39), channel_id=1, replica_groups=mesh['kpt'=4,'pw'=8] {'pw'}, use_global_device_ids=true, to_apply=%region_21.0 | all-reduce | flops 6 | bytes 48 | tf_op jit(solution)/shard_map/psum | solution.py:56
  256.2 14.2 %all_gather.33 = bf16[2,4,512]{1,0,2:T(2,128)(2,1)S(1)} all-gather(bf16[2,4,64]{1,0,2:T(2,128)(2,1)S(1)} %copy.43), channel_id=1, replica_groups=mesh['kpt'=4,'pw'=8] {'pw'}, dimensions={2}, use_global_device_ids=true | all-gather | bytes 9216 | tf_op jit(solution)/shard_map/all_gather | solution.py:35
  271.0 7.3 %all_gather.34 = bf16[16,2,512]{2,1,0:T(2,128)(2,1)S(1)} all-gather(bf16[4,2,512]{2,1,0:T(2,128)(2,1)S(1)} %convolution_convert_fusion), channel_id=1, replica_groups=mesh['kpt'=4,'pw'=8] {'kpt'}, dimensions={0}, use_global_device_ids=true | all-gather | bytes 40960 | tf_op jit(solution)/shard_map/all_gather | solution.py:11
  278.3 14.2 %all_gather.35 = bf16[16,2,4096]{2,0,1:T(8,128)(2,1)S(1)} all-gather(bf16[16,2,512]{2,0,1:T(8,128)(2,1)S(1)} %copy.45), channel_id=1, replica_groups=mesh['kpt'=4,'pw'=8] {'pw'}, dimensions={2}, use_global_device_ids=true | all-gather | bytes 294912 | tf_op jit(solution)/shard_map/all_gather | solution.py:15
  292.5 10.8 %fusion.12 = f32[4,16,2,512]{3,1,0,2:T(8,128)S(1)} fusion(bf16[4,512,4096]{2,1,0:T(8,128)(2,1)} %param.14, bf16[16,2,4096]{2,0,1:T(8,128)(2,1)S(1)} %all_gather.35), kind=kOutput, calls=%fused_computation.8 | convolution fusion | flops 536870912 | bytes 17301504 | tf_op jit(solution)/shard_map/qsg,kvg->qkvs/dot_general | solution.py:12
  303.7 16.2 %all-reduce.2 = bf16[16,2,512]{2,1,0:T(2,128)(2,1)S(1)} all-reduce(f32[16,2,512]{2,1,0:T(2,128)S(1)} %copy.46), channel_id=6, replica_groups=mesh['kpt'=4,'pw'=8] {'kpt'}, use_global_device_ids=true, to_apply=%region_22.0.clone | all-reduce | flops 16384 | bytes 98304
  323.7 28.1 %reduce-scatter.14.cloned.1.call-done = f32[64,8]{1,0:T(8,128)} async-done(((f32[512,8]{1,0:T(8,128)}), f32[64,8]{1,0:T(8,128)}) %reduce-scatter.14.cloned.1.call-update) | async-done | bytes 2064
  353.0 9.9 %all-reduce.6 = (f32[2]{0:T(128)S(1)}, f32[2]{0:T(128)S(1)}, f32[2]{0:T(128)S(1)}) all-reduce(f32[2]{0:T(128)S(1)} %get-tuple-element.18, f32[2]{0:T(128)S(1)} %get-tuple-element.17, f32[2]{0:T(128)S(1)} %get-tuple-element.16), channel_id=1, replica_groups=mesh['kpt'=4,'pw'=8] {'kpt'}, use_global_device_ids=true, to_apply=%region_31.0 | all-reduce | flops 6 | bytes 48 | tf_op jit(solution)/shard_map/psum | solution.py:57
  362.9 13.6 %all-reduce.3 = (f32[2]{0:T(128)S(1)}, f32[2]{0:T(128)S(1)}, f32[2]{0:T(128)S(1)}) all-reduce(f32[2]{0:T(128)S(1)} %get-tuple-element.34, f32[2]{0:T(128)S(1)} %get-tuple-element.35, f32[2]{0:T(128)S(1)} %get-tuple-element.36), channel_id=1, replica_groups=mesh['kpt'=4,'pw'=8] {'pw'}, use_global_device_ids=true, to_apply=%region_32.0 | all-reduce | flops 6 | bytes 48 | tf_op jit(solution)/shard_map/psum | solution.py:56
  (71 shorter events, 22.0 us)
Async XLA Ops:
  7.2 17.1 %copy-start = (bf16[4,512,512]{2,1,0:T(8,128)(2,1)S(1)}, bf16[4,512,512]{2,1,0:T(8,128)(2,1)}, u32[]{:S(2)}) copy-start(bf16[4,512,512]{2,1,0:T(8,128)(2,1)} %param.13) | copy-start | bytes 6291460
  7.2 103.6 %reduce-scatter.10.cloned.1.call-start = ((), (), s32[]{:S(2)}) async-start(), calls=%async_computation.3 | async-start | bytes 294912
  47.2 10.8 %copy-start.1 = (s32[16,16]{1,0:T(8,128)S(1)}, s32[16,16]{1,0:T(8,128)}, u32[]{:S(2)}) copy-start(s32[16,16]{1,0:T(8,128)} %param.15) | copy-start | bytes 3076
  47.2 27.3 %copy-start.7 = (u32[32]{0:T(128)S(1)}, u32[32]{0:T(128)}, u32[]{:S(2)}) copy-start(u32[32]{0:T(128)} %constant.29) | copy-start | bytes 388
  75.7 36.0 %copy-start.2 = (f32[2,4,64]{2,1,0:T(4,128)S(1)}, f32[2,4,64]{2,1,0:T(4,128)}, u32[]{:S(2)}) copy-start(f32[2,4,64]{2,1,0:T(4,128)} %param.9) | copy-start | bytes 6148
  75.7 36.0 %copy-start.4 = (f32[4,64]{1,0:T(4,128)S(1)}, f32[4,64]{1,0:T(4,128)}, u32[]{:S(2)}) copy-start(f32[4,64]{1,0:T(4,128)} %param.8) | copy-start | bytes 3076
  75.8 36.0 %copy-start.5 = (f32[2,4,64]{2,1,0:T(4,128)S(1)}, f32[2,4,64]{2,1,0:T(4,128)}, u32[]{:S(2)}) copy-start(f32[2,4,64]{2,1,0:T(4,128)} %param.10) | copy-start | bytes 6148
  75.8 36.0 %copy-start.6 = (f32[2]{0:T(128)S(1)}, f32[2]{0:T(128)}, u32[]{:S(2)}) copy-start(f32[2]{0:T(128)} %param.11) | copy-start | bytes 28
  79.6 151.8 %reduce-scatter.12.cloned.1.call-start = ((), (), s32[]{:S(2)}) async-start(), calls=%async_computation.4 | async-start | bytes 294912
  203.3 148.6 %reduce-scatter.14.cloned.1.call-start = ((), (), s32[]{:S(2)}) async-start(), calls=%async_computation.5 | async-start | bytes 294912
  256.1 121.7 %copy-start.3 = (f32[2,4,64]{2,1,0:T(4,128)}, f32[2,4,64]{2,1,0:T(4,128)S(1)}, u32[]{:S(2)}) copy-start(f32[2,4,64]{2,1,0:T(4,128)S(1)} %get-tuple-element.45) | copy-start | bytes 6148
Sparse Core Ops, SparseCore 0:
  79.8 30.9 reduce-scatter.9
  203.4 28.0 reduce-scatter.11
  323.9 27.9 reduce-scatter.13
